TPU v7x, 128 devices: a whole 4x4x4 slice. The times are simulated.
128 devices in a mesh: prow: 8 (over y, core), pcol: 16 (over z, x).
Axes of the slice: x: 4, y: 4, z: 4, core: 2. Of those that a mesh axis runs over, the one named last changes fastest.
Arguments:
- inverse_cov: bfloat16 [8192, 8192], P('prow', 'pcol'), may hold values from -0.5 to 4.5, as said below
- cosines: float32 [8192, 8192], P('prow', 'pcol'), may hold values from -1 to 1, as said below
- sky_maps: bfloat16 [8192, 192], P('pcol'), may hold values from -6 to 6
Outputs:
- filtered: bfloat16 [8192, 192], P('prow')
- spectra: float32 [64, 192], replicated
Inputs may be any that keep to these rules, and one draw needn't show every extreme that they name: `inverse_cov`: symmetric, with a dominant diagonal. `cosines`: symmetric.
All inputs are finite; a program needn't handle non-finite values.
Results may differ from a plain program's by a relative error of at most 0.0033.
Values may be sent and summed in bfloat16 or wider, within the bound.
No kernel may reach another device: no remote copies, remote signals or barrier semaphores. Data moves between devices by JAX's collectives and lax.ppermute only.
A program may use at most 64 MiB of HBM per device.

v0:
```python
import jax
import jax.numpy as jnp
from jax import lax
from jax.sharding import Mesh
from jax.sharding import PartitionSpec as P

NPIX = 8192
L = 64
LMIN = 2
GROUP = 4
PCOL = ("pcol_0", "pcol_1")
PROW = ("prow_0", "prow_1")
PROW_PCOL = ("prow_0", "prow_1", "pcol_0", "pcol_1")


def split_up(value, dim, length):
    dims = value.shape
    parts = value.reshape(*dims[:dim], length, dims[dim] // length, *dims[dim + 1 :])
    return jnp.moveaxis(parts, dim, 0)


def summed_on_arrival(value, axis, dim):
    length = lax.axis_size(axis)
    parts = lax.all_to_all(split_up(value, dim, length), axis, 0, 0, tiled=True)
    return jnp.sum(parts, axis=0)


def from_everyone(value, axis):
    length = lax.axis_size(axis)
    return lax.all_to_all(
        jnp.broadcast_to(value[None], (length, *value.shape)), axis, 0, 0, tiled=True
    )


def joined_along(parts, dim):
    parts = jnp.moveaxis(parts, 0, dim)
    dims = parts.shape
    return parts.reshape(*dims[:dim], dims[dim] * dims[dim + 1], *dims[dim + 2 :])


def collect(value, axis, dim):
    parts = from_everyone(value, axis)
    return joined_along(parts, dim)


def broadcast(value, axis, root):
    return lax.dynamic_index_in_dim(lax.all_gather(value, axis), root, 0, keepdims=False)


def by_axis(value, axes):
    for axis in axes:
        value = lax.psum(value, axis)
    return value


def next_legendre(previous, current, cosine, degree):
    return ((2.0 * degree - 1.0) * cosine * current - (degree - 1.0) * previous) / degree


def per_device(inverse_cov, cosines, sky_maps):
    cols_here = inverse_cov.shape[1]
    own_rows = summed_on_arrival(
        jnp.dot(inverse_cov, sky_maps, preferred_element_type=jnp.float32), PCOL, 0
    ).astype(jnp.bfloat16)
    filtered = collect(own_rows, PCOL, 0)
    column_index = lax.axis_index(PCOL)
    col_ratio = lax.axis_size(PCOL) // lax.axis_size(PROW)
    owner_row = column_index // col_ratio
    source = broadcast(filtered, PROW, owner_row)
    filtered_cols = lax.dynamic_slice_in_dim(
        source, column_index % col_ratio * cols_here, cols_here, 0
    )
    rows_f32 = filtered.astype(jnp.float32)
    previous = jnp.ones_like(cosines)
    current = cosines

    def advance(carried, turn_index):
        previous, current = carried
        term_list = []
        weights = []
        for offset in range(GROUP):
            degree = (LMIN + turn_index * GROUP + offset).astype(jnp.float32)
            next_term = next_legendre(previous, current, cosines, degree)
            term_list.append(next_term.astype(jnp.bfloat16))
            weights.append((2.0 * degree + 1.0) / NPIX)
            previous, current = (current, next_term)
        stacked = jnp.stack(term_list)
        product = jnp.einsum(
            "grc,cm->grm", stacked, filtered_cols, preferred_element_type=jnp.float32
        )
        quadratic = jnp.sum(product * rows_f32[None], axis=1)
        return ((previous, current), quadratic * jnp.stack(weights)[:, None])

    carried, partial_spectra = lax.scan(
        advance, (previous, current), jnp.arange(L // GROUP, dtype=jnp.int32)
    )
    spectra = by_axis(partial_spectra.reshape(L, -1), PROW_PCOL)
    return (filtered, spectra)


def solution(mesh):
    split = Mesh(mesh.devices.reshape(4, 2, 4, 4), ("prow_0", "prow_1", "pcol_0", "pcol_1"))
    placed = (P(PROW, PCOL), P(PROW, PCOL), P(PCOL, None))
    return jax.shard_map(
        per_device, mesh=split, in_specs=placed, out_specs=(P(PROW, None), P()), check_vma=False
    )
```

profile of v0, /device:TPU:0, one launch (start us, length us, event | category | flops | bytes accessed | tf_op | source)
XLA Modules:
  0.0 353.4 jit_solution(7335706579062819510)
XLA Ops:
  9.8 24.9 %all_to_all.10 = f32[16,64,192]{2,1,0:T(8,128)S(1)} all-to-all(f32[16,64,192]{2,1,0:T(8,128)S(1)} %bitcast.57), channel_id=1, replica_groups=mesh['prow_0'=4,'prow_1'=2,'pcol_0'=4,'pcol_1'=4] {'pcol_0','pcol_1'}, dimensions={0} | all-to-all | bytes 1572864 | tf_op jit(solution)/shard_map/all_to_all | solution.py:24
  34.8 13.7 %all_to_all.11 = bf16[16,64,192]{2,1,0:T(8,128)(2,1)S(1)} all-to-all(bf16[16,64,192]{2,1,0:T(8,128)(2,1)S(1)} %broadcast_in_dim.7), channel_id=1, replica_groups=mesh['prow_0'=4,'prow_1'=2,'pcol_0'=4,'pcol_1'=4] {'pcol_0','pcol_1'}, dimensions={0} | all-to-all | bytes 786432 | tf_op jit(solution)/shard_map/all_to_all | solution.py:30
  55.3 19.7 %all-gather.2.cloned.1.call-done = bf16[8,1024,192]{1,2,0:T(8,128)(2,1)} async-done(((bf16[1,1024,192]{1,2,0:T(8,128)(2,1)}), bf16[8,1024,192]{1,2,0:T(8,128)(2,1)}) %all-gather.2.cloned.1.call-update) | async-done | bytes 3145744 | tf_op jit(solution)/shard_map/all_gather | solution.py:47
  76.1 214.6 %while.18 = (s32[]{:T(128)}, f32[1024,512]{1,0:T(8,128)}, f32[1024,512]{1,0:T(8,128)S(1)}, f32[16,4,192]{2,1,0:T(4,128)S(1)}, s32[16]{0:T(128)S(1)}, /*index=5*/...) while((s32[]{:T(128)}, f32[1024,512]{1,0:T(8,128)}, ...), condition=%wide.region_3.4_spmd.clone, body=%wide.region_1.3_spmd.clone.sunk | while | flops 832045056 | bytes 69153048 | solution.py:94
  90.4 4.2 %convert_bitcast_fusion.6 = (bf16[1,1024,512]{2,1,0:T(8,128)(2,1)S(1)}, f32[1024,512]{1,0:T(8,128)S(1)}, bf16[1,1024,512]{2,1,0:T(8,128)(2,1)S(1)}) fusion(f32[]{:T(128)} %bitcast.47, f32[]{:T(128)S(6)} %sub.103, f32[]{:T(128)} %bitcast.48, f32[1024,512]{1,0:T(8,128)} %copy-done.2, f32[]{:T(128)S(6)} %sub.104, f32[]{:T(128)} %bitcast.49, ...), kind=kLoop, calls=%fused_computation.16.clone.1 | loop fusion | flops 9437184 | bytes 10485797 | tf_op jit(solution)/shard_map/while/body/eval_jaxpr/stack | solution.py:87
  94.6 4.1 %convert_bitcast_fusion.7 = (bf16[1,1024,512]{2,1,0:T(8,128)(2,1)S(1)}, f32[1024,512]{1,0:T(8,128)}, bf16[1,1024,512]{2,1,0:T(8,128)(2,1)S(1)}) fusion(f32[]{:T(128)} %bitcast.50, f32[]{:T(128)} %bitcast.48, f32[1024,512]{1,0:T(8,128)} %copy-done.2, f32[]{:T(128)S(6)} %sub.104, f32[]{:T(128)} %bitcast.49, f32[1024,512]{1,0:T(8,128)S(1)} %copy-done.5, ...), kind=kLoop, calls=%fused_computation.15.clone.1 | loop fusion | flops 9437184 | bytes 12582949 | tf_op jit(solution)/shard_map/while/body/eval_jaxpr/stack | solution.py:87
  103.8 4.2 %convert_bitcast_fusion.6 = (bf16[1,1024,512]{2,1,0:T(8,128)(2,1)S(1)}, f32[1024,512]{1,0:T(8,128)S(1)}, bf16[1,1024,512]{2,1,0:T(8,128)(2,1)S(1)}) fusion(f32[]{:T(128)} %bitcast.47, f32[]{:T(128)S(6)} %sub.103, f32[]{:T(128)} %bitcast.48, f32[1024,512]{1,0:T(8,128)} %copy-done.2, f32[]{:T(128)S(6)} %sub.104, f32[]{:T(128)} %bitcast.49, ...), kind=kLoop, calls=%fused_computation.16.clone.1 | loop fusion | flops 9437184 | bytes 10485797 | tf_op jit(solution)/shard_map/while/body/eval_jaxpr/stack | solution.py:87
  108.0 4.1 %convert_bitcast_fusion.7 = (bf16[1,1024,512]{2,1,0:T(8,128)(2,1)S(1)}, f32[1024,512]{1,0:T(8,128)}, bf16[1,1024,512]{2,1,0:T(8,128)(2,1)S(1)}) fusion(f32[]{:T(128)} %bitcast.50, f32[]{:T(128)} %bitcast.48, f32[1024,512]{1,0:T(8,128)} %copy-done.2, f32[]{:T(128)S(6)} %sub.104, f32[]{:T(128)} %bitcast.49, f32[1024,512]{1,0:T(8,128)S(1)} %copy-done.5, ...), kind=kLoop, calls=%fused_computation.15.clone.1 | loop fusion | flops 9437184 | bytes 12582949 | tf_op jit(solution)/shard_map/while/body/eval_jaxpr/stack | solution.py:87
  117.3 4.2 %convert_bitcast_fusion.6 = (bf16[1,1024,512]{2,1,0:T(8,128)(2,1)S(1)}, f32[1024,512]{1,0:T(8,128)S(1)}, bf16[1,1024,512]{2,1,0:T(8,128)(2,1)S(1)}) fusion(f32[]{:T(128)} %bitcast.47, f32[]{:T(128)S(6)} %sub.103, f32[]{:T(128)} %bitcast.48, f32[1024,512]{1,0:T(8,128)} %copy-done.2, f32[]{:T(128)S(6)} %sub.104, f32[]{:T(128)} %bitcast.49, ...), kind=kLoop, calls=%fused_computation.16.clone.1 | loop fusion | flops 9437184 | bytes 10485797 | tf_op jit(solution)/shard_map/while/body/eval_jaxpr/stack | solution.py:87
  130.7 4.2 %convert_bitcast_fusion.6 = (bf16[1,1024,512]{2,1,0:T(8,128)(2,1)S(1)}, f32[1024,512]{1,0:T(8,128)S(1)}, bf16[1,1024,512]{2,1,0:T(8,128)(2,1)S(1)}) fusion(f32[]{:T(128)} %bitcast.47, f32[]{:T(128)S(6)} %sub.103, f32[]{:T(128)} %bitcast.48, f32[1024,512]{1,0:T(8,128)} %copy-done.2, f32[]{:T(128)S(6)} %sub.104, f32[]{:T(128)} %bitcast.49, ...), kind=kLoop, calls=%fused_computation.16.clone.1 | loop fusion | flops 9437184 | bytes 10485797 | tf_op jit(solution)/shard_map/while/body/eval_jaxpr/stack | solution.py:87
  144.2 4.2 %convert_bitcast_fusion.6 = (bf16[1,1024,512]{2,1,0:T(8,128)(2,1)S(1)}, f32[1024,512]{1,0:T(8,128)S(1)}, bf16[1,1024,512]{2,1,0:T(8,128)(2,1)S(1)}) fusion(f32[]{:T(128)} %bitcast.47, f32[]{:T(128)S(6)} %sub.103, f32[]{:T(128)} %bitcast.48, f32[1024,512]{1,0:T(8,128)} %copy-done.2, f32[]{:T(128)S(6)} %sub.104, f32[]{:T(128)} %bitcast.49, ...), kind=kLoop, calls=%fused_computation.16.clone.1 | loop fusion | flops 9437184 | bytes 10485797 | tf_op jit(solution)/shard_map/while/body/eval_jaxpr/stack | solution.py:87
  157.6 4.2 %convert_bitcast_fusion.6 = (bf16[1,1024,512]{2,1,0:T(8,128)(2,1)S(1)}, f32[1024,512]{1,0:T(8,128)S(1)}, bf16[1,1024,512]{2,1,0:T(8,128)(2,1)S(1)}) fusion(f32[]{:T(128)} %bitcast.47, f32[]{:T(128)S(6)} %sub.103, f32[]{:T(128)} %bitcast.48, f32[1024,512]{1,0:T(8,128)} %copy-done.2, f32[]{:T(128)S(6)} %sub.104, f32[]{:T(128)} %bitcast.49, ...), kind=kLoop, calls=%fused_computation.16.clone.1 | loop fusion | flops 9437184 | bytes 10485797 | tf_op jit(solution)/shard_map/while/body/eval_jaxpr/stack | solution.py:87
  171.1 4.2 %convert_bitcast_fusion.6 = (bf16[1,1024,512]{2,1,0:T(8,128)(2,1)S(1)}, f32[1024,512]{1,0:T(8,128)S(1)}, bf16[1,1024,512]{2,1,0:T(8,128)(2,1)S(1)}) fusion(f32[]{:T(128)} %bitcast.47, f32[]{:T(128)S(6)} %sub.103, f32[]{:T(128)} %bitcast.48, f32[1024,512]{1,0:T(8,128)} %copy-done.2, f32[]{:T(128)S(6)} %sub.104, f32[]{:T(128)} %bitcast.49, ...), kind=kLoop, calls=%fused_computation.16.clone.1 | loop fusion | flops 9437184 | bytes 10485797 | tf_op jit(solution)/shard_map/while/body/eval_jaxpr/stack | solution.py:87
  184.5 4.2 %convert_bitcast_fusion.6 = (bf16[1,1024,512]{2,1,0:T(8,128)(2,1)S(1)}, f32[1024,512]{1,0:T(8,128)S(1)}, bf16[1,1024,512]{2,1,0:T(8,128)(2,1)S(1)}) fusion(f32[]{:T(128)} %bitcast.47, f32[]{:T(128)S(6)} %sub.103, f32[]{:T(128)} %bitcast.48, f32[1024,512]{1,0:T(8,128)} %copy-done.2, f32[]{:T(128)S(6)} %sub.104, f32[]{:T(128)} %bitcast.49, ...), kind=kLoop, calls=%fused_computation.16.clone.1 | loop fusion | flops 9437184 | bytes 10485797 | tf_op jit(solution)/shard_map/while/body/eval_jaxpr/stack | solution.py:87
  198.0 4.2 %convert_bitcast_fusion.6 = (bf16[1,1024,512]{2,1,0:T(8,128)(2,1)S(1)}, f32[1024,512]{1,0:T(8,128)S(1)}, bf16[1,1024,512]{2,1,0:T(8,128)(2,1)S(1)}) fusion(f32[]{:T(128)} %bitcast.47, f32[]{:T(128)S(6)} %sub.103, f32[]{:T(128)} %bitcast.48, f32[1024,512]{1,0:T(8,128)} %copy-done.2, f32[]{:T(128)S(6)} %sub.104, f32[]{:T(128)} %bitcast.49, ...), kind=kLoop, calls=%fused_computation.16.clone.1 | loop fusion | flops 9437184 | bytes 10485797 | tf_op jit(solution)/shard_map/while/body/eval_jaxpr/stack | solution.py:87
  211.4 4.2 %convert_bitcast_fusion.6 = (bf16[1,1024,512]{2,1,0:T(8,128)(2,1)S(1)}, f32[1024,512]{1,0:T(8,128)S(1)}, bf16[1,1024,512]{2,1,0:T(8,128)(2,1)S(1)}) fusion(f32[]{:T(128)} %bitcast.47, f32[]{:T(128)S(6)} %sub.103, f32[]{:T(128)} %bitcast.48, f32[1024,512]{1,0:T(8,128)} %copy-done.2, f32[]{:T(128)S(6)} %sub.104, f32[]{:T(128)} %bitcast.49, ...), kind=kLoop, calls=%fused_computation.16.clone.1 | loop fusion | flops 9437184 | bytes 10485797 | tf_op jit(solution)/shard_map/while/body/eval_jaxpr/stack | solution.py:87
  224.9 4.2 %convert_bitcast_fusion.6 = (bf16[1,1024,512]{2,1,0:T(8,128)(2,1)S(1)}, f32[1024,512]{1,0:T(8,128)S(1)}, bf16[1,1024,512]{2,1,0:T(8,128)(2,1)S(1)}) fusion(f32[]{:T(128)} %bitcast.47, f32[]{:T(128)S(6)} %sub.103, f32[]{:T(128)} %bitcast.48, f32[1024,512]{1,0:T(8,128)} %copy-done.2, f32[]{:T(128)S(6)} %sub.104, f32[]{:T(128)} %bitcast.49, ...), kind=kLoop, calls=%fused_computation.16.clone.1 | loop fusion | flops 9437184 | bytes 10485797 | tf_op jit(solution)/shard_map/while/body/eval_jaxpr/stack | solution.py:87
  238.3 4.2 %convert_bitcast_fusion.6 = (bf16[1,1024,512]{2,1,0:T(8,128)(2,1)S(1)}, f32[1024,512]{1,0:T(8,128)S(1)}, bf16[1,1024,512]{2,1,0:T(8,128)(2,1)S(1)}) fusion(f32[]{:T(128)} %bitcast.47, f32[]{:T(128)S(6)} %sub.103, f32[]{:T(128)} %bitcast.48, f32[1024,512]{1,0:T(8,128)} %copy-done.2, f32[]{:T(128)S(6)} %sub.104, f32[]{:T(128)} %bitcast.49, ...), kind=kLoop, calls=%fused_computation.16.clone.1 | loop fusion | flops 9437184 | bytes 10485797 | tf_op jit(solution)/shard_map/while/body/eval_jaxpr/stack | solution.py:87
  251.8 4.2 %convert_bitcast_fusion.6 = (bf16[1,1024,512]{2,1,0:T(8,128)(2,1)S(1)}, f32[1024,512]{1,0:T(8,128)S(1)}, bf16[1,1024,512]{2,1,0:T(8,128)(2,1)S(1)}) fusion(f32[]{:T(128)} %bitcast.47, f32[]{:T(128)S(6)} %sub.103, f32[]{:T(128)} %bitcast.48, f32[1024,512]{1,0:T(8,128)} %copy-done.2, f32[]{:T(128)S(6)} %sub.104, f32[]{:T(128)} %bitcast.49, ...), kind=kLoop, calls=%fused_computation.16.clone.1 | loop fusion | flops 9437184 | bytes 10485797 | tf_op jit(solution)/shard_map/while/body/eval_jaxpr/stack | solution.py:87
  265.2 4.2 %convert_bitcast_fusion.6 = (bf16[1,1024,512]{2,1,0:T(8,128)(2,1)S(1)}, f32[1024,512]{1,0:T(8,128)S(1)}, bf16[1,1024,512]{2,1,0:T(8,128)(2,1)S(1)}) fusion(f32[]{:T(128)} %bitcast.47, f32[]{:T(128)S(6)} %sub.103, f32[]{:T(128)} %bitcast.48, f32[1024,512]{1,0:T(8,128)} %copy-done.2, f32[]{:T(128)S(6)} %sub.104, f32[]{:T(128)} %bitcast.49, ...), kind=kLoop, calls=%fused_computation.16.clone.1 | loop fusion | flops 9437184 | bytes 10485797 | tf_op jit(solution)/shard_map/while/body/eval_jaxpr/stack | solution.py:87
  278.6 4.2 %convert_bitcast_fusion.6 = (bf16[1,1024,512]{2,1,0:T(8,128)(2,1)S(1)}, f32[1024,512]{1,0:T(8,128)S(1)}, bf16[1,1024,512]{2,1,0:T(8,128)(2,1)S(1)}) fusion(f32[]{:T(128)} %bitcast.47, f32[]{:T(128)S(6)} %sub.103, f32[]{:T(128)} %bitcast.48, f32[1024,512]{1,0:T(8,128)} %copy-done.2, f32[]{:T(128)S(6)} %sub.104, f32[]{:T(128)} %bitcast.49, ...), kind=kLoop, calls=%fused_computation.16.clone.1 | loop fusion | flops 9437184 | bytes 10485797 | tf_op jit(solution)/shard_map/while/body/eval_jaxpr/stack | solution.py:87
  290.7 16.5 %psum.28 = f32[64,192]{1,0:T(8,128)S(1)} all-reduce(f32[64,192]{1,0:T(8,128)S(1)} %reshape.63), channel_id=1, replica_groups=mesh['prow_0'=4,'prow_1'=2,'pcol_0'=4,'pcol_1'=4] {'prow_0'}, use_global_device_ids=true, to_apply=%region_4.5 | all-reduce | flops 12288 | bytes 98304 | tf_op jit(solution)/shard_map/psum | solution.py:52
  310.8 17.7 %psum.30 = f32[64,192]{1,0:T(8,128)S(1)} all-reduce(f32[64,192]{1,0:T(8,128)S(1)} %psum.29), channel_id=1, replica_groups=mesh['prow_0'=4,'prow_1'=2,'pcol_0'=4,'pcol_1'=4] {'pcol_0'}, use_global_device_ids=true, to_apply=%region_6.7 | all-reduce | flops 12288 | bytes 98304 | tf_op jit(solution)/shard_map/psum | solution.py:52
  328.5 18.0 %psum.31 = f32[64,192]{1,0:T(8,128)} all-reduce(f32[64,192]{1,0:T(8,128)S(1)} %psum.30), channel_id=1, replica_groups=mesh['prow_0'=4,'prow_1'=2,'pcol_0'=4,'pcol_1'=4] {'pcol_1'}, use_global_device_ids=true, to_apply=%region_7.8 | all-reduce | flops 12288 | bytes 98304 | tf_op jit(solution)/shard_map/psum | solution.py:52
  (276 shorter events, 146.6 us)
Async XLA Ops:
  7.2 67.8 %all-gather.2.cloned.1.call-start = ((), (), s32[]{:S(2)}) async-start(), calls=%async_computation.2 | async-start | bytes 3538944 | tf_op jit(solution)/shard_map/all_gather | solution.py:47
  50.6 25.5 %copy-start.4 = (f32[1024,512]{1,0:T(8,128)S(1)}, f32[1024,512]{1,0:T(8,128)}, u32[]{:S(2)}) copy-start(f32[1024,512]{1,0:T(8,128)} %param.6) | copy-start | bytes 6291460
  90.4 4.2 %copy-start.1 = (f32[1024,512]{1,0:T(8,128)S(1)}, f32[1024,512]{1,0:T(8,128)}, u32[]{:S(2)}) copy-start(f32[1024,512]{1,0:T(8,128)} %get-tuple-element.322) | copy-start | bytes 6291460 | tf_op jit(solution)/shard_map/while
  90.4 4.2 %copy-start.5 = (f32[1024,512]{1,0:T(8,128)S(1)}, f32[1024,512]{1,0:T(8,128)}, u32[]{:S(2)}) copy-start(f32[1024,512]{1,0:T(8,128)} %get-tuple-element.300) | copy-start | bytes 6291460 | tf_op jit(solution)/shard_map/while
  103.8 4.2 %copy-start.1 = (f32[1024,512]{1,0:T(8,128)S(1)}, f32[1024,512]{1,0:T(8,128)}, u32[]{:S(2)}) copy-start(f32[1024,512]{1,0:T(8,128)} %get-tuple-element.322) | copy-start | bytes 6291460 | tf_op jit(solution)/shard_map/while
  103.8 4.2 %copy-start.5 = (f32[1024,512]{1,0:T(8,128)S(1)}, f32[1024,512]{1,0:T(8,128)}, u32[]{:S(2)}) copy-start(f32[1024,512]{1,0:T(8,128)} %get-tuple-element.300) | copy-start | bytes 6291460 | tf_op jit(solution)/shard_map/while
  117.3 4.2 %copy-start.1 = (f32[1024,512]{1,0:T(8,128)S(1)}, f32[1024,512]{1,0:T(8,128)}, u32[]{:S(2)}) copy-start(f32[1024,512]{1,0:T(8,128)} %get-tuple-element.322) | copy-start | bytes 6291460 | tf_op jit(solution)/shard_map/while
  117.3 4.2 %copy-start.5 = (f32[1024,512]{1,0:T(8,128)S(1)}, f32[1024,512]{1,0:T(8,128)}, u32[]{:S(2)}) copy-start(f32[1024,512]{1,0:T(8,128)} %get-tuple-element.300) | copy-start | bytes 6291460 | tf_op jit(solution)/shard_map/while
  130.7 4.2 %copy-start.1 = (f32[1024,512]{1,0:T(8,128)S(1)}, f32[1024,512]{1,0:T(8,128)}, u32[]{:S(2)}) copy-start(f32[1024,512]{1,0:T(8,128)} %get-tuple-element.322) | copy-start | bytes 6291460 | tf_op jit(solution)/shard_map/while
  130.7 4.2 %copy-start.5 = (f32[1024,512]{1,0:T(8,128)S(1)}, f32[1024,512]{1,0:T(8,128)}, u32[]{:S(2)}) copy-start(f32[1024,512]{1,0:T(8,128)} %get-tuple-element.300) | copy-start | bytes 6291460 | tf_op jit(solution)/shard_map/while
  144.2 4.2 %copy-start.1 = (f32[1024,512]{1,0:T(8,128)S(1)}, f32[1024,512]{1,0:T(8,128)}, u32[]{:S(2)}) copy-start(f32[1024,512]{1,0:T(8,128)} %get-tuple-element.322) | copy-start | bytes 6291460 | tf_op jit(solution)/shard_map/while
  144.2 4.2 %copy-start.5 = (f32[1024,512]{1,0:T(8,128)S(1)}, f32[1024,512]{1,0:T(8,128)}, u32[]{:S(2)}) copy-start(f32[1024,512]{1,0:T(8,128)} %get-tuple-element.300) | copy-start | bytes 6291460 | tf_op jit(solution)/shard_map/while
  157.6 4.2 %copy-start.1 = (f32[1024,512]{1,0:T(8,128)S(1)}, f32[1024,512]{1,0:T(8,128)}, u32[]{:S(2)}) copy-start(f32[1024,512]{1,0:T(8,128)} %get-tuple-element.322) | copy-start | bytes 6291460 | tf_op jit(solution)/shard_map/while
  157.6 4.2 %copy-start.5 = (f32[1024,512]{1,0:T(8,128)S(1)}, f32[1024,512]{1,0:T(8,128)}, u32[]{:S(2)}) copy-start(f32[1024,512]{1,0:T(8,128)} %get-tuple-element.300) | copy-start | bytes 6291460 | tf_op jit(solution)/shard_map/while
  171.1 4.2 %copy-start.1 = (f32[1024,512]{1,0:T(8,128)S(1)}, f32[1024,512]{1,0:T(8,128)}, u32[]{:S(2)}) copy-start(f32[1024,512]{1,0:T(8,128)} %get-tuple-element.322) | copy-start | bytes 6291460 | tf_op jit(solution)/shard_map/while
  171.1 4.2 %copy-start.5 = (f32[1024,512]{1,0:T(8,128)S(1)}, f32[1024,512]{1,0:T(8,128)}, u32[]{:S(2)}) copy-start(f32[1024,512]{1,0:T(8,128)} %get-tuple-element.300) | copy-start | bytes 6291460 | tf_op jit(solution)/shard_map/while
  184.5 4.2 %copy-start.5 = (f32[1024,512]{1,0:T(8,128)S(1)}, f32[1024,512]{1,0:T(8,128)}, u32[]{:S(2)}) copy-start(f32[1024,512]{1,0:T(8,128)} %get-tuple-element.300) | copy-start | bytes 6291460 | tf_op jit(solution)/shard_map/while
  198.0 4.2 %copy-start.5 = (f32[1024,512]{1,0:T(8,128)S(1)}, f32[1024,512]{1,0:T(8,128)}, u32[]{:S(2)}) copy-start(f32[1024,512]{1,0:T(8,128)} %get-tuple-element.300) | copy-start | bytes 6291460 | tf_op jit(solution)/shard_map/while
  211.4 4.2 %copy-start.5 = (f32[1024,512]{1,0:T(8,128)S(1)}, f32[1024,512]{1,0:T(8,128)}, u32[]{:S(2)}) copy-start(f32[1024,512]{1,0:T(8,128)} %get-tuple-element.300) | copy-start | bytes 6291460 | tf_op jit(solution)/shard_map/while
  224.8 4.2 %copy-start.5 = (f32[1024,512]{1,0:T(8,128)S(1)}, f32[1024,512]{1,0:T(8,128)}, u32[]{:S(2)}) copy-start(f32[1024,512]{1,0:T(8,128)} %get-tuple-element.300) | copy-start | bytes 6291460 | tf_op jit(solution)/shard_map/while
  238.3 4.2 %copy-start.5 = (f32[1024,512]{1,0:T(8,128)S(1)}, f32[1024,512]{1,0:T(8,128)}, u32[]{:S(2)}) copy-start(f32[1024,512]{1,0:T(8,128)} %get-tuple-element.300) | copy-start | bytes 6291460 | tf_op jit(solution)/shard_map/while
  251.7 4.2 %copy-start.5 = (f32[1024,512]{1,0:T(8,128)S(1)}, f32[1024,512]{1,0:T(8,128)}, u32[]{:S(2)}) copy-start(f32[1024,512]{1,0:T(8,128)} %get-tuple-element.300) | copy-start | bytes 6291460 | tf_op jit(solution)/shard_map/while
  265.2 4.2 %copy-start.5 = (f32[1024,512]{1,0:T(8,128)S(1)}, f32[1024,512]{1,0:T(8,128)}, u32[]{:S(2)}) copy-start(f32[1024,512]{1,0:T(8,128)} %get-tuple-element.300) | copy-start | bytes 6291460 | tf_op jit(solution)/shard_map/while
  278.6 4.2 %copy-start.5 = (f32[1024,512]{1,0:T(8,128)S(1)}, f32[1024,512]{1,0:T(8,128)}, u32[]{:S(2)}) copy-start(f32[1024,512]{1,0:T(8,128)} %get-tuple-element.300) | copy-start | bytes 6291460 | tf_op jit(solution)/shard_map/while
  (60 other events, 124.6 us)
Sparse Core Ops, SparseCore 0:
  49.7 25.3 all-gather.1
where the time goes:
time: 355 us; the launch traced here: 353 us
  other arithmetic  137 us (39%)
  blocking collectives  94.5 us (27%)
  local copies, waits for them, and re-layouts  44.7 us (13%)
  matrix products  32 us (9%)
  waiting for transfers between devices  19.8 us (6%)
  between operations  14.2 us (4%)
  loops' own time  11.1 us (3%)
    another operation x32, other arithmetic, advance(): stacked = jnp.stack(term_list)  132 us
    psum x4, blocking collectives, by_axis(): value = lax.psum(value, axis)  55.8 us
    dot_general x16, matrix products, advance(): jnp.einsum('grc,cm->grm', stacked, filtered_cols, preferred_element_type=...  30.6 us
    while x176, local copies, waits for them, and re-layouts  27.1 us
    all_to_all x1, blocking collectives, summed_on_arrival(): parts = lax.all_to_all(split_up(value, dim, length), axis, 0, 0, tiled=True)  24.9 us
    all_gather x1, waiting for transfers between devices, broadcast(): lax.all_gather(value, axis)  19.7 us
    all_to_all x1, blocking collectives, from_everyone(): lax.all_to_all(jnp.broadcast_to(value[None], (length, *value.shape)), axi...  13.7 us
    another operation x1, loops' own time, per_device(): lax.scan(advance, (previous, current), jnp.arange(L // GROUP, dtype=jnp.i...  11.1 us
  transfers between devices with their start and end apart: 1, of which 1 were waited for; matrix products, arithmetic and copies ran while one was open for 2% of the time, Pallas kernels for 0%

commit v1 on v0

--- a/solution.py
+++ b/solution.py
@@ -49,7 +49,7 @@
 
 def by_axis(value, axes):
     for axis in axes:
-        value = lax.psum(value, axis)
+        value = jnp.sum(lax.all_gather(value, axis), axis=0)
     return value
 
 

time: 355 us -> 340 us (0.958)
  blocking collectives: 94.5 us -> 78.4 us
    psum x4 -> x0, blocking collectives: 55.8 us -> none  [by_axis(): value = lax.psum(value, axis)]
    all_gather x0 -> x4, blocking collectives: none -> 39.7 us  [by_axis(): value = jnp.sum(lax.all_gather(value, axis), axis=0)]
where the time goes in v1:
time: 340 us; the launch traced here: 338 us
  other arithmetic  138 us (41%)
  blocking collectives  78.4 us (23%)
  local copies, waits for them, and re-layouts  44.7 us (13%)
  matrix products  32 us (9%)
  waiting for transfers between devices  19.8 us (6%)
  between operations  14.2 us (4%)
  loops' own time  11.1 us (3%)
    another operation x32, other arithmetic, advance(): stacked = jnp.stack(term_list)  132 us
    all_gather x4, blocking collectives, by_axis(): value = jnp.sum(lax.all_gather(value, axis), axis=0)  39.7 us
    dot_general x16, matrix products, advance(): jnp.einsum('grc,cm->grm', stacked, filtered_cols, preferred_element_type=...  30.6 us
    while x176, local copies, waits for them, and re-layouts  27.1 us
    all_to_all x1, blocking collectives, summed_on_arrival(): parts = lax.all_to_all(split_up(value, dim, length), axis, 0, 0, tiled=True)  24.9 us
    all_gather x1, waiting for transfers between devices, broadcast(): lax.all_gather(value, axis)  19.7 us
    all_to_all x1, blocking collectives, from_everyone(): lax.all_to_all(jnp.broadcast_to(value[None], (length, *value.shape)), axi...  13.7 us
    another operation x1, loops' own time, per_device(): lax.scan(advance, (previous, current), jnp.arange(L // GROUP, dtype=jnp.i...  11.1 us
  transfers between devices with their start and end apart: 1, of which 1 were waited for; matrix products, arithmetic and copies ran while one was open for 2% of the time, Pallas kernels for 0%

profile of v1, /device:TPU:0, one launch (start us, length us, event | category | flops | bytes accessed | tf_op | source)
XLA Modules:
  0.0 337.9 jit_solution(14711332085989907678)
XLA Ops:
  9.8 24.9 %all_to_all.10 = f32[16,64,192]{2,1,0:T(8,128)S(1)} all-to-all(f32[16,64,192]{2,1,0:T(8,128)S(1)} %bitcast.60), channel_id=1, replica_groups=mesh['prow_0'=4,'prow_1'=2,'pcol_0'=4,'pcol_1'=4] {'pcol_0','pcol_1'}, dimensions={0} | all-to-all | bytes 1572864 | tf_op jit(solution)/shard_map/all_to_all | solution.py:24
  34.8 13.7 %all_to_all.11 = bf16[16,64,192]{2,1,0:T(8,128)(2,1)S(1)} all-to-all(bf16[16,64,192]{2,1,0:T(8,128)(2,1)S(1)} %broadcast_in_dim.7), channel_id=1, replica_groups=mesh['prow_0'=4,'prow_1'=2,'pcol_0'=4,'pcol_1'=4] {'pcol_0','pcol_1'}, dimensions={0} | all-to-all | bytes 786432 | tf_op jit(solution)/shard_map/all_to_all | solution.py:30
  55.3 19.7 %all-gather.5.cloned.1.call-done = bf16[8,1024,192]{1,2,0:T(8,128)(2,1)} async-done(((bf16[1,1024,192]{1,2,0:T(8,128)(2,1)}), bf16[8,1024,192]{1,2,0:T(8,128)(2,1)}) %all-gather.5.cloned.1.call-update) | async-done | bytes 3145744 | tf_op jit(solution)/shard_map/all_gather | solution.py:47
  76.1 214.6 %while.18 = (s32[]{:T(128)}, f32[1024,512]{1,0:T(8,128)}, f32[1024,512]{1,0:T(8,128)S(1)}, f32[16,4,192]{2,1,0:T(4,128)S(1)}, s32[16]{0:T(128)S(1)}, /*index=5*/...) while((s32[]{:T(128)}, f32[1024,512]{1,0:T(8,128)}, ...), condition=%wide.region_3.4_spmd.clone, body=%wide.region_1.3_spmd.clone.sunk | while | flops 832045056 | bytes 69153048 | solution.py:94
  81.1 4.1 %convert_bitcast_fusion.7 = (bf16[1,1024,512]{2,1,0:T(8,128)(2,1)S(1)}, f32[1024,512]{1,0:T(8,128)}, bf16[1,1024,512]{2,1,0:T(8,128)(2,1)S(1)}) fusion(f32[]{:T(128)} %bitcast.53, f32[]{:T(128)} %bitcast.51, f32[1024,512]{1,0:T(8,128)} %copy-done.2, f32[]{:T(128)S(6)} %sub.104, f32[]{:T(128)} %bitcast.52, f32[1024,512]{1,0:T(8,128)S(1)} %copy-done.5, ...), kind=kLoop, calls=%fused_computation.15.clone.1 | loop fusion | flops 9437184 | bytes 12582949 | tf_op jit(solution)/shard_map/while/body/eval_jaxpr/stack | solution.py:87
  90.4 4.2 %convert_bitcast_fusion.6 = (bf16[1,1024,512]{2,1,0:T(8,128)(2,1)S(1)}, f32[1024,512]{1,0:T(8,128)S(1)}, bf16[1,1024,512]{2,1,0:T(8,128)(2,1)S(1)}) fusion(f32[]{:T(128)} %bitcast.50, f32[]{:T(128)S(6)} %sub.103, f32[]{:T(128)} %bitcast.51, f32[1024,512]{1,0:T(8,128)} %copy-done.2, f32[]{:T(128)S(6)} %sub.104, f32[]{:T(128)} %bitcast.52, ...), kind=kLoop, calls=%fused_computation.16.clone.1 | loop fusion | flops 9437184 | bytes 10485797 | tf_op jit(solution)/shard_map/while/body/eval_jaxpr/stack | solution.py:87
  94.6 4.1 %convert_bitcast_fusion.7 = (bf16[1,1024,512]{2,1,0:T(8,128)(2,1)S(1)}, f32[1024,512]{1,0:T(8,128)}, bf16[1,1024,512]{2,1,0:T(8,128)(2,1)S(1)}) fusion(f32[]{:T(128)} %bitcast.53, f32[]{:T(128)} %bitcast.51, f32[1024,512]{1,0:T(8,128)} %copy-done.2, f32[]{:T(128)S(6)} %sub.104, f32[]{:T(128)} %bitcast.52, f32[1024,512]{1,0:T(8,128)S(1)} %copy-done.5, ...), kind=kLoop, calls=%fused_computation.15.clone.1 | loop fusion | flops 9437184 | bytes 12582949 | tf_op jit(solution)/shard_map/while/body/eval_jaxpr/stack | solution.py:87
  103.8 4.2 %convert_bitcast_fusion.6 = (bf16[1,1024,512]{2,1,0:T(8,128)(2,1)S(1)}, f32[1024,512]{1,0:T(8,128)S(1)}, bf16[1,1024,512]{2,1,0:T(8,128)(2,1)S(1)}) fusion(f32[]{:T(128)} %bitcast.50, f32[]{:T(128)S(6)} %sub.103, f32[]{:T(128)} %bitcast.51, f32[1024,512]{1,0:T(8,128)} %copy-done.2, f32[]{:T(128)S(6)} %sub.104, f32[]{:T(128)} %bitcast.52, ...), kind=kLoop, calls=%fused_computation.16.clone.1 | loop fusion | flops 9437184 | bytes 10485797 | tf_op jit(solution)/shard_map/while/body/eval_jaxpr/stack | solution.py:87
  117.3 4.2 %convert_bitcast_fusion.6 = (bf16[1,1024,512]{2,1,0:T(8,128)(2,1)S(1)}, f32[1024,512]{1,0:T(8,128)S(1)}, bf16[1,1024,512]{2,1,0:T(8,128)(2,1)S(1)}) fusion(f32[]{:T(128)} %bitcast.50, f32[]{:T(128)S(6)} %sub.103, f32[]{:T(128)} %bitcast.51, f32[1024,512]{1,0:T(8,128)} %copy-done.2, f32[]{:T(128)S(6)} %sub.104, f32[]{:T(128)} %bitcast.52, ...), kind=kLoop, calls=%fused_computation.16.clone.1 | loop fusion | flops 9437184 | bytes 10485797 | tf_op jit(solution)/shard_map/while/body/eval_jaxpr/stack | solution.py:87
  130.7 4.2 %convert_bitcast_fusion.6 = (bf16[1,1024,512]{2,1,0:T(8,128)(2,1)S(1)}, f32[1024,512]{1,0:T(8,128)S(1)}, bf16[1,1024,512]{2,1,0:T(8,128)(2,1)S(1)}) fusion(f32[]{:T(128)} %bitcast.50, f32[]{:T(128)S(6)} %sub.103, f32[]{:T(128)} %bitcast.51, f32[1024,512]{1,0:T(8,128)} %copy-done.2, f32[]{:T(128)S(6)} %sub.104, f32[]{:T(128)} %bitcast.52, ...), kind=kLoop, calls=%fused_computation.16.clone.1 | loop fusion | flops 9437184 | bytes 10485797 | tf_op jit(solution)/shard_map/while/body/eval_jaxpr/stack | solution.py:87
  144.2 4.2 %convert_bitcast_fusion.6 = (bf16[1,1024,512]{2,1,0:T(8,128)(2,1)S(1)}, f32[1024,512]{1,0:T(8,128)S(1)}, bf16[1,1024,512]{2,1,0:T(8,128)(2,1)S(1)}) fusion(f32[]{:T(128)} %bitcast.50, f32[]{:T(128)S(6)} %sub.103, f32[]{:T(128)} %bitcast.51, f32[1024,512]{1,0:T(8,128)} %copy-done.2, f32[]{:T(128)S(6)} %sub.104, f32[]{:T(128)} %bitcast.52, ...), kind=kLoop, calls=%fused_computation.16.clone.1 | loop fusion | flops 9437184 | bytes 10485797 | tf_op jit(solution)/shard_map/while/body/eval_jaxpr/stack | solution.py:87
  157.6 4.2 %convert_bitcast_fusion.6 = (bf16[1,1024,512]{2,1,0:T(8,128)(2,1)S(1)}, f32[1024,512]{1,0:T(8,128)S(1)}, bf16[1,1024,512]{2,1,0:T(8,128)(2,1)S(1)}) fusion(f32[]{:T(128)} %bitcast.50, f32[]{:T(128)S(6)} %sub.103, f32[]{:T(128)} %bitcast.51, f32[1024,512]{1,0:T(8,128)} %copy-done.2, f32[]{:T(128)S(6)} %sub.104, f32[]{:T(128)} %bitcast.52, ...), kind=kLoop, calls=%fused_computation.16.clone.1 | loop fusion | flops 9437184 | bytes 10485797 | tf_op jit(solution)/shard_map/while/body/eval_jaxpr/stack | solution.py:87
  171.1 4.2 %convert_bitcast_fusion.6 = (bf16[1,1024,512]{2,1,0:T(8,128)(2,1)S(1)}, f32[1024,512]{1,0:T(8,128)S(1)}, bf16[1,1024,512]{2,1,0:T(8,128)(2,1)S(1)}) fusion(f32[]{:T(128)} %bitcast.50, f32[]{:T(128)S(6)} %sub.103, f32[]{:T(128)} %bitcast.51, f32[1024,512]{1,0:T(8,128)} %copy-done.2, f32[]{:T(128)S(6)} %sub.104, f32[]{:T(128)} %bitcast.52, ...), kind=kLoop, calls=%fused_computation.16.clone.1 | loop fusion | flops 9437184 | bytes 10485797 | tf_op jit(solution)/shard_map/while/body/eval_jaxpr/stack | solution.py:87
  184.5 4.2 %convert_bitcast_fusion.6 = (bf16[1,1024,512]{2,1,0:T(8,128)(2,1)S(1)}, f32[1024,512]{1,0:T(8,128)S(1)}, bf16[1,1024,512]{2,1,0:T(8,128)(2,1)S(1)}) fusion(f32[]{:T(128)} %bitcast.50, f32[]{:T(128)S(6)} %sub.103, f32[]{:T(128)} %bitcast.51, f32[1024,512]{1,0:T(8,128)} %copy-done.2, f32[]{:T(128)S(6)} %sub.104, f32[]{:T(128)} %bitcast.52, ...), kind=kLoop, calls=%fused_computation.16.clone.1 | loop fusion | flops 9437184 | bytes 10485797 | tf_op jit(solution)/shard_map/while/body/eval_jaxpr/stack | solution.py:87
  198.0 4.2 %convert_bitcast_fusion.6 = (bf16[1,1024,512]{2,1,0:T(8,128)(2,1)S(1)}, f32[1024,512]{1,0:T(8,128)S(1)}, bf16[1,1024,512]{2,1,0:T(8,128)(2,1)S(1)}) fusion(f32[]{:T(128)} %bitcast.50, f32[]{:T(128)S(6)} %sub.103, f32[]{:T(128)} %bitcast.51, f32[1024,512]{1,0:T(8,128)} %copy-done.2, f32[]{:T(128)S(6)} %sub.104, f32[]{:T(128)} %bitcast.52, ...), kind=kLoop, calls=%fused_computation.16.clone.1 | loop fusion | flops 9437184 | bytes 10485797 | tf_op jit(solution)/shard_map/while/body/eval_jaxpr/stack | solution.py:87
  211.4 4.2 %convert_bitcast_fusion.6 = (bf16[1,1024,512]{2,1,0:T(8,128)(2,1)S(1)}, f32[1024,512]{1,0:T(8,128)S(1)}, bf16[1,1024,512]{2,1,0:T(8,128)(2,1)S(1)}) fusion(f32[]{:T(128)} %bitcast.50, f32[]{:T(128)S(6)} %sub.103, f32[]{:T(128)} %bitcast.51, f32[1024,512]{1,0:T(8,128)} %copy-done.2, f32[]{:T(128)S(6)} %sub.104, f32[]{:T(128)} %bitcast.52, ...), kind=kLoop, calls=%fused_computation.16.clone.1 | loop fusion | flops 9437184 | bytes 10485797 | tf_op jit(solution)/shard_map/while/body/eval_jaxpr/stack | solution.py:87
  224.9 4.2 %convert_bitcast_fusion.6 = (bf16[1,1024,512]{2,1,0:T(8,128)(2,1)S(1)}, f32[1024,512]{1,0:T(8,128)S(1)}, bf16[1,1024,512]{2,1,0:T(8,128)(2,1)S(1)}) fusion(f32[]{:T(128)} %bitcast.50, f32[]{:T(128)S(6)} %sub.103, f32[]{:T(128)} %bitcast.51, f32[1024,512]{1,0:T(8,128)} %copy-done.2, f32[]{:T(128)S(6)} %sub.104, f32[]{:T(128)} %bitcast.52, ...), kind=kLoop, calls=%fused_computation.16.clone.1 | loop fusion | flops 9437184 | bytes 10485797 | tf_op jit(solution)/shard_map/while/body/eval_jaxpr/stack | solution.py:87
  238.3 4.2 %convert_bitcast_fusion.6 = (bf16[1,1024,512]{2,1,0:T(8,128)(2,1)S(1)}, f32[1024,512]{1,0:T(8,128)S(1)}, bf16[1,1024,512]{2,1,0:T(8,128)(2,1)S(1)}) fusion(f32[]{:T(128)} %bitcast.50, f32[]{:T(128)S(6)} %sub.103, f32[]{:T(128)} %bitcast.51, f32[1024,512]{1,0:T(8,128)} %copy-done.2, f32[]{:T(128)S(6)} %sub.104, f32[]{:T(128)} %bitcast.52, ...), kind=kLoop, calls=%fused_computation.16.clone.1 | loop fusion | flops 9437184 | bytes 10485797 | tf_op jit(solution)/shard_map/while/body/eval_jaxpr/stack | solution.py:87
  251.8 4.2 %convert_bitcast_fusion.6 = (bf16[1,1024,512]{2,1,0:T(8,128)(2,1)S(1)}, f32[1024,512]{1,0:T(8,128)S(1)}, bf16[1,1024,512]{2,1,0:T(8,128)(2,1)S(1)}) fusion(f32[]{:T(128)} %bitcast.50, f32[]{:T(128)S(6)} %sub.103, f32[]{:T(128)} %bitcast.51, f32[1024,512]{1,0:T(8,128)} %copy-done.2, f32[]{:T(128)S(6)} %sub.104, f32[]{:T(128)} %bitcast.52, ...), kind=kLoop, calls=%fused_computation.16.clone.1 | loop fusion | flops 9437184 | bytes 10485797 | tf_op jit(solution)/shard_map/while/body/eval_jaxpr/stack | solution.py:87
  265.2 4.2 %convert_bitcast_fusion.6 = (bf16[1,1024,512]{2,1,0:T(8,128)(2,1)S(1)}, f32[1024,512]{1,0:T(8,128)S(1)}, bf16[1,1024,512]{2,1,0:T(8,128)(2,1)S(1)}) fusion(f32[]{:T(128)} %bitcast.50, f32[]{:T(128)S(6)} %sub.103, f32[]{:T(128)} %bitcast.51, f32[1024,512]{1,0:T(8,128)} %copy-done.2, f32[]{:T(128)S(6)} %sub.104, f32[]{:T(128)} %bitcast.52, ...), kind=kLoop, calls=%fused_computation.16.clone.1 | loop fusion | flops 9437184 | bytes 10485797 | tf_op jit(solution)/shard_map/while/body/eval_jaxpr/stack | solution.py:87
  278.6 4.2 %convert_bitcast_fusion.6 = (bf16[1,1024,512]{2,1,0:T(8,128)(2,1)S(1)}, f32[1024,512]{1,0:T(8,128)S(1)}, bf16[1,1024,512]{2,1,0:T(8,128)(2,1)S(1)}) fusion(f32[]{:T(128)} %bitcast.50, f32[]{:T(128)S(6)} %sub.103, f32[]{:T(128)} %bitcast.51, f32[1024,512]{1,0:T(8,128)} %copy-done.2, f32[]{:T(128)S(6)} %sub.104, f32[]{:T(128)} %bitcast.52, ...), kind=kLoop, calls=%fused_computation.16.clone.1 | loop fusion | flops 9437184 | bytes 10485797 | tf_op jit(solution)/shard_map/while/body/eval_jaxpr/stack | solution.py:87
  290.7 12.3 %all_gather.25 = f32[4,64,192]{2,1,0:T(8,128)S(1)} all-gather(f32[1,64,192]{2,1,0:T(8,128)S(1)} %all_gather_reshape.7), channel_id=1, replica_groups=mesh['prow_0'=4,'prow_1'=2,'pcol_0'=4,'pcol_1'=4] {'prow_0'}, dimensions={0}, use_global_device_ids=true | all-gather | bytes 245760 | tf_op jit(solution)/shard_map/all_gather | solution.py:52
  304.9 12.7 %all-gather.1 = f32[256,192]{1,0:T(8,128)S(1)} all-gather(f32[64,192]{1,0:T(8,128)S(1)} %reduce_sum.62), channel_id=3, replica_groups=mesh['prow_0'=4,'prow_1'=2,'pcol_0'=4,'pcol_1'=4] {'pcol_0'}, dimensions={0}, use_global_device_ids=true | all-gather | bytes 245760 | tf_op jit(solution)/shard_map/all_gather | solution.py:52
  317.7 12.8 %all-gather.2 = f32[256,192]{1,0:T(8,128)S(1)} all-gather(f32[64,192]{1,0:T(8,128)S(1)} %reduce_sum.63), channel_id=4, replica_groups=mesh['prow_0'=4,'prow_1'=2,'pcol_0'=4,'pcol_1'=4] {'pcol_1'}, dimensions={0}, use_global_device_ids=true | all-gather | bytes 245760 | tf_op jit(solution)/shard_map/all_gather | solution.py:52
  (280 shorter events, 145.6 us)
Async XLA Ops:
  7.2 67.8 %all-gather.5.cloned.1.call-start = ((), (), s32[]{:S(2)}) async-start(), calls=%async_computation.2 | async-start | bytes 3538944 | tf_op jit(solution)/shard_map/all_gather | solution.py:47
  50.6 25.5 %copy-start.4 = (f32[1024,512]{1,0:T(8,128)S(1)}, f32[1024,512]{1,0:T(8,128)}, u32[]{:S(2)}) copy-start(f32[1024,512]{1,0:T(8,128)} %param.6) | copy-start | bytes 6291460
  90.4 4.2 %copy-start.1 = (f32[1024,512]{1,0:T(8,128)S(1)}, f32[1024,512]{1,0:T(8,128)}, u32[]{:S(2)}) copy-start(f32[1024,512]{1,0:T(8,128)} %get-tuple-element.332) | copy-start | bytes 6291460 | tf_op jit(solution)/shard_map/while
  90.4 4.2 %copy-start.5 = (f32[1024,512]{1,0:T(8,128)S(1)}, f32[1024,512]{1,0:T(8,128)}, u32[]{:S(2)}) copy-start(f32[1024,512]{1,0:T(8,128)} %get-tuple-element.310) | copy-start | bytes 6291460 | tf_op jit(solution)/shard_map/while
  103.8 4.2 %copy-start.1 = (f32[1024,512]{1,0:T(8,128)S(1)}, f32[1024,512]{1,0:T(8,128)}, u32[]{:S(2)}) copy-start(f32[1024,512]{1,0:T(8,128)} %get-tuple-element.332) | copy-start | bytes 6291460 | tf_op jit(solution)/shard_map/while
  103.8 4.2 %copy-start.5 = (f32[1024,512]{1,0:T(8,128)S(1)}, f32[1024,512]{1,0:T(8,128)}, u32[]{:S(2)}) copy-start(f32[1024,512]{1,0:T(8,128)} %get-tuple-element.310) | copy-start | bytes 6291460 | tf_op jit(solution)/shard_map/while
  117.3 4.2 %copy-start.1 = (f32[1024,512]{1,0:T(8,128)S(1)}, f32[1024,512]{1,0:T(8,128)}, u32[]{:S(2)}) copy-start(f32[1024,512]{1,0:T(8,128)} %get-tuple-element.332) | copy-start | bytes 6291460 | tf_op jit(solution)/shard_map/while
  117.3 4.2 %copy-start.5 = (f32[1024,512]{1,0:T(8,128)S(1)}, f32[1024,512]{1,0:T(8,128)}, u32[]{:S(2)}) copy-start(f32[1024,512]{1,0:T(8,128)} %get-tuple-element.310) | copy-start | bytes 6291460 | tf_op jit(solution)/shard_map/while
  130.7 4.2 %copy-start.1 = (f32[1024,512]{1,0:T(8,128)S(1)}, f32[1024,512]{1,0:T(8,128)}, u32[]{:S(2)}) copy-start(f32[1024,512]{1,0:T(8,128)} %get-tuple-element.332) | copy-start | bytes 6291460 | tf_op jit(solution)/shard_map/while
  130.7 4.2 %copy-start.5 = (f32[1024,512]{1,0:T(8,128)S(1)}, f32[1024,512]{1,0:T(8,128)}, u32[]{:S(2)}) copy-start(f32[1024,512]{1,0:T(8,128)} %get-tuple-element.310) | copy-start | bytes 6291460 | tf_op jit(solution)/shard_map/while
  144.2 4.2 %copy-start.1 = (f32[1024,512]{1,0:T(8,128)S(1)}, f32[1024,512]{1,0:T(8,128)}, u32[]{:S(2)}) copy-start(f32[1024,512]{1,0:T(8,128)} %get-tuple-element.332) | copy-start | bytes 6291460 | tf_op jit(solution)/shard_map/while
  144.2 4.2 %copy-start.5 = (f32[1024,512]{1,0:T(8,128)S(1)}, f32[1024,512]{1,0:T(8,128)}, u32[]{:S(2)}) copy-start(f32[1024,512]{1,0:T(8,128)} %get-tuple-element.310) | copy-start | bytes 6291460 | tf_op jit(solution)/shard_map/while
  157.6 4.2 %copy-start.1 = (f32[1024,512]{1,0:T(8,128)S(1)}, f32[1024,512]{1,0:T(8,128)}, u32[]{:S(2)}) copy-start(f32[1024,512]{1,0:T(8,128)} %get-tuple-element.332) | copy-start | bytes 6291460 | tf_op jit(solution)/shard_map/while
  157.6 4.2 %copy-start.5 = (f32[1024,512]{1,0:T(8,128)S(1)}, f32[1024,512]{1,0:T(8,128)}, u32[]{:S(2)}) copy-start(f32[1024,512]{1,0:T(8,128)} %get-tuple-element.310) | copy-start | bytes 6291460 | tf_op jit(solution)/shard_map/while
  171.1 4.2 %copy-start.1 = (f32[1024,512]{1,0:T(8,128)S(1)}, f32[1024,512]{1,0:T(8,128)}, u32[]{:S(2)}) copy-start(f32[1024,512]{1,0:T(8,128)} %get-tuple-element.332) | copy-start | bytes 6291460 | tf_op jit(solution)/shard_map/while
  171.1 4.2 %copy-start.5 = (f32[1024,512]{1,0:T(8,128)S(1)}, f32[1024,512]{1,0:T(8,128)}, u32[]{:S(2)}) copy-start(f32[1024,512]{1,0:T(8,128)} %get-tuple-element.310) | copy-start | bytes 6291460 | tf_op jit(solution)/shard_map/while
  184.5 4.2 %copy-start.5 = (f32[1024,512]{1,0:T(8,128)S(1)}, f32[1024,512]{1,0:T(8,128)}, u32[]{:S(2)}) copy-start(f32[1024,512]{1,0:T(8,128)} %get-tuple-element.310) | copy-start | bytes 6291460 | tf_op jit(solution)/shard_map/while
  198.0 4.2 %copy-start.5 = (f32[1024,512]{1,0:T(8,128)S(1)}, f32[1024,512]{1,0:T(8,128)}, u32[]{:S(2)}) copy-start(f32[1024,512]{1,0:T(8,128)} %get-tuple-element.310) | copy-start | bytes 6291460 | tf_op jit(solution)/shard_map/while
  211.4 4.2 %copy-start.5 = (f32[1024,512]{1,0:T(8,128)S(1)}, f32[1024,512]{1,0:T(8,128)}, u32[]{:S(2)}) copy-start(f32[1024,512]{1,0:T(8,128)} %get-tuple-element.310) | copy-start | bytes 6291460 | tf_op jit(solution)/shard_map/while
  224.8 4.2 %copy-start.5 = (f32[1024,512]{1,0:T(8,128)S(1)}, f32[1024,512]{1,0:T(8,128)}, u32[]{:S(2)}) copy-start(f32[1024,512]{1,0:T(8,128)} %get-tuple-element.310) | copy-start | bytes 6291460 | tf_op jit(solution)/shard_map/while
  238.3 4.2 %copy-start.5 = (f32[1024,512]{1,0:T(8,128)S(1)}, f32[1024,512]{1,0:T(8,128)}, u32[]{:S(2)}) copy-start(f32[1024,512]{1,0:T(8,128)} %get-tuple-element.310) | copy-start | bytes 6291460 | tf_op jit(solution)/shard_map/while
  251.7 4.2 %copy-start.5 = (f32[1024,512]{1,0:T(8,128)S(1)}, f32[1024,512]{1,0:T(8,128)}, u32[]{:S(2)}) copy-start(f32[1024,512]{1,0:T(8,128)} %get-tuple-element.310) | copy-start | bytes 6291460 | tf_op jit(solution)/shard_map/while
  265.2 4.2 %copy-start.5 = (f32[1024,512]{1,0:T(8,128)S(1)}, f32[1024,512]{1,0:T(8,128)}, u32[]{:S(2)}) copy-start(f32[1024,512]{1,0:T(8,128)} %get-tuple-element.310) | copy-start | bytes 6291460 | tf_op jit(solution)/shard_map/while
  278.6 4.2 %copy-start.5 = (f32[1024,512]{1,0:T(8,128)S(1)}, f32[1024,512]{1,0:T(8,128)}, u32[]{:S(2)}) copy-start(f32[1024,512]{1,0:T(8,128)} %get-tuple-element.310) | copy-start | bytes 6291460 | tf_op jit(solution)/shard_map/while
  (60 other events, 124.6 us)
Sparse Core Ops, SparseCore 0:
  49.7 25.3 all-gather.4
